TPU v7x, 32 devices: a whole 2x2x4 slice. The times are simulated.
32 devices in a mesh: leaf: 16 (over z, y, x), tile: 2 (over core).
Axes of the slice: x: 2, y: 2, z: 4, core: 2. Of those that a mesh axis runs over, the one named last changes fastest.
Arguments:
- rhs: float32 [5, 64, 8, 128], P(None, ('leaf', 'tile')), may hold values from -6 to 6
- lower: bfloat16 [4, 64, 3, 128, 128], P(None, ('leaf', 'tile')), may hold values from -0.21875 to 0.21875
- upper: bfloat16 [4, 64, 3, 128, 128], P(None, ('leaf', 'tile')), may hold values from -0.21875 to 0.21875
- diag_inv: bfloat16 [5, 64, 128, 128], P(None, ('leaf', 'tile')), may hold values from -0.4 to 1.4
- pattern: int32 [4, 64, 3], replicated, may hold values from 0 to 63, as said below
- counts: int32 [5, 32], P(None, ('leaf', 'tile')), may hold values from 1 to 2
- basis: float32 [8, 5, 64, 8, 128], P(None, None, ('leaf', 'tile')), may hold values from -1 to 1, as said below
Outputs:
- precond: float32 [5, 64, 8, 128], P(None, ('leaf', 'tile'))
- coeffs: float32 [9, 8], replicated
Inputs may be any that keep to these rules, and one draw needn't show every extreme that they name: `pattern`: the entries of level index i (connector level i + 1) lie below 2 ** (i + 2) * 2: tiles of the level below within the same group, numbered device by device and slot by slot. `counts`: slots 0 to count - 1 of a device at a level hold tiles; the other slots are empty. `basis`: for each right-hand side the 8 vectors are orthonormal over all unknowns.
All inputs are finite; a program needn't handle non-finite values.
Results may differ from a plain program's by a relative error of at most 0.009.
Values may be sent and summed in bfloat16 or wider, within the bound.
A program may use at most 64 MiB of HBM per device.

v0:
```python
import math

import jax
import jax.numpy as jnp
from jax import lax
from jax.sharding import PartitionSpec as P

epsilon = 1e-06


def partner_2(shard, axis, bit):
    return lax.ppermute(shard, axis, [(i, i ^ 1 << bit) for i in range(lax.axis_size(axis))])


def forward_gather(buffer, level_index):
    partner = partner_2(buffer, "tile", 0)
    lower_core = lax.axis_index("tile") == 0
    buffer = jnp.where(
        lower_core, jnp.concatenate([buffer, partner], 0), jnp.concatenate([partner, buffer], 0)
    )
    leaf_index = lax.axis_index("leaf")
    for bit_index in range(level_index):
        partner = partner_2(buffer, "leaf", bit_index)
        bit_clear = leaf_index // 2**bit_index % 2 == 0
        buffer = jnp.where(
            bit_clear, jnp.concatenate([buffer, partner], 0), jnp.concatenate([partner, buffer], 0)
        )
    return buffer


def products_gather(buffer, level_index):
    partner = partner_2(buffer, "tile", 0)
    lower_core = lax.axis_index("tile") == 0
    buffer = jnp.where(
        lower_core, jnp.concatenate([buffer, partner], 0), jnp.concatenate([partner, buffer], 0)
    )
    leaf_index = lax.axis_index("leaf")
    for bit_index in range(level_index):
        partner = partner_2(buffer, "leaf", bit_index)
        bit_clear = leaf_index // 2**bit_index % 2 == 0
        buffer = jnp.where(
            bit_clear, jnp.concatenate([buffer, partner], 0), jnp.concatenate([partner, buffer], 0)
        )
    return buffer


def local(rhs, lower, upper, diag_inv, pattern, counts, basis):
    levels, tiles_dev, columns, tile_rows = rhs.shape
    neighbours = lower.shape[2]
    device = lax.axis_index("leaf") * lax.axis_size("tile") + lax.axis_index("tile")
    live_mask = (lax.iota(jnp.int32, tiles_dev)[None, :] < counts).astype(jnp.float32)[
        :, :, None, None
    ]
    own_pattern = lax.dynamic_slice_in_dim(pattern, device * tiles_dev, tiles_dev, 1)
    forward_vals = [live_mask[0] * rhs[0]]
    for level_index in range(1, levels):
        grouped = forward_gather(forward_vals[-1].astype(jnp.bfloat16), level_index)
        picked = grouped[own_pattern[level_index - 1]]
        coupling = jnp.einsum(
            "tnab,tnrb->tra", lower[level_index - 1], picked, preferred_element_type=jnp.float32
        )
        forward_vals.append(live_mask[level_index] * (rhs[level_index] - coupling))
    solutions = [None] * levels
    upstream = jnp.zeros_like(rhs[0])
    for level_index in reversed(range(levels)):
        operand = (forward_vals[level_index] - upstream).astype(jnp.bfloat16)
        solution = live_mask[level_index] * jnp.einsum(
            "tab,trb->tra", diag_inv[level_index], operand, preferred_element_type=jnp.float32
        )
        solutions[level_index] = solution
        if level_index > 0:
            products = jnp.einsum(
                "tnab,trb->tnra",
                upper[level_index - 1],
                solution.astype(jnp.bfloat16),
                preferred_element_type=jnp.float32,
            )
            span = 2 ** (level_index + 1)
            group_tiles = span * tiles_dev
            group_start = device // span * span
            gathered = products_gather(products, level_index)
            group_pattern = lax.dynamic_slice_in_dim(
                pattern[level_index - 1], group_start * tiles_dev, group_tiles, 0
            ).reshape(-1)
            my_slots = (device - group_start) * tiles_dev + lax.iota(jnp.int32, tiles_dev)
            onehot = (my_slots[:, None] == group_pattern[None, :]).astype(jnp.float32)
            flat = gathered.reshape(group_tiles * neighbours, columns * tile_rows)
            received = jnp.dot(
                onehot, flat, precision=lax.Precision.HIGHEST, preferred_element_type=jnp.float32
            )
            upstream = received.reshape(tiles_dev, columns, tile_rows)
    precond = jnp.stack(solutions, 0)
    local_proj = jnp.einsum("mltrb,ltrb->mr", basis, precond, precision=lax.Precision.HIGHEST)
    projections, total_sq = lax.psum(
        (local_proj, jnp.sum(precond * precond, axis=(0, 1, 3))), ("leaf", "tile")
    )
    squared = total_sq - jnp.sum(projections * projections, axis=0)
    length_norm = jnp.sqrt(squared + epsilon)
    total_rows = levels * tiles_dev * tile_rows * lax.axis_size("leaf") * lax.axis_size("tile")
    scaled = length_norm / math.sqrt(total_rows)
    coeffs = jnp.concatenate([projections, scaled[None, :]], 0)
    return (precond, coeffs)


def solution(mesh):
    return jax.shard_map(
        local,
        mesh=mesh,
        in_specs=(
            P(None, ("leaf", "tile"), None, None),
            P(None, ("leaf", "tile"), None, None, None),
            P(None, ("leaf", "tile"), None, None, None),
            P(None, ("leaf", "tile"), None, None),
            P(),
            P(None, ("leaf", "tile")),
            P(None, None, ("leaf", "tile"), None, None),
        ),
        out_specs=(P(None, ("leaf", "tile"), None, None), P()),
        check_vma=False,
    )
```

profile of v0, /device:TPU:0, one launch (start us, length us, event | category | flops | bytes accessed | tf_op | source)
XLA Modules:
  0.0 161.6 jit_solution(895148639310521065)
XLA Ops:
  0.7 0.7 copy-done.7
  1.4 0.8 fusion.60
  2.2 0.5 collective-permute-start
  2.7 0.9 constant_dynamic-slice_fusion.5
  3.9 2.5 %collective-permute-start.1 = (bf16[4,8,128]{2,1,0:T(8,128)(2,1)S(1)}, bf16[4,8,128]{2,1,0:T(8,128)(2,1)S(1)}, u32[]{:S(2)}, u32[]{:S(2)}) collective-permute-start(bf16[4,8,128]{2,1,0:T(8,128)(2,1)S(1)} %maximum_select_fusion.24), channel_id=1, source_target_pairs={{0,2},{2,0},{4,6},{6,4},{8,10},{10,8},{12,14},{14,12},{16,18},{18,... | collective-permute-start | bytes 24584 | tf_op jit(solution)/shard_map/ppermute | solution.py:12
  6.4 1.6 %collective-permute-done.1 = bf16[4,8,128]{2,1,0:T(8,128)(2,1)S(1)} collective-permute-done((bf16[4,8,128]{2,1,0:T(8,128)(2,1)S(1)}, bf16[4,8,128]{2,1,0:T(8,128)(2,1)S(1)}, u32[]{:S(2)}, u32[]{:S(2)}) %collective-permute-start.1) | collective-permute-done | bytes 8224 | tf_op jit(solution)/shard_map/ppermute | solution.py:12
  8.1 0.6 gather_fusion
  8.6 1.1 fusion.93
  9.7 1.2 collective-permute-done.2
  10.9 2.0 %collective-permute-start.3 = (bf16[4,8,128]{2,1,0:T(8,128)(2,1)S(1)}, bf16[4,8,128]{2,1,0:T(8,128)(2,1)S(1)}, u32[]{:S(2)}, u32[]{:S(2)}) collective-permute-start(bf16[4,8,128]{2,1,0:T(8,128)(2,1)S(1)} %maximum_select_fusion.25), channel_id=1, source_target_pairs={{0,2},{2,0},{4,6},{6,4},{8,10},{10,8},{12,14},{14,12},{16,18},{18,... | collective-permute-start | bytes 24584 | tf_op jit(solution)/shard_map/ppermute | solution.py:12
  13.0 1.5 collective-permute-done.3
  14.6 2.0 %collective-permute-start.4 = (bf16[8,8,128]{2,1,0:T(8,128)(2,1)S(1)}, bf16[8,8,128]{2,1,0:T(8,128)(2,1)S(1)}, u32[]{:S(2)}, u32[]{:S(2)}) collective-permute-start(bf16[8,8,128]{2,1,0:T(8,128)(2,1)S(1)} %maximum_select_fusion.21), channel_id=1, source_target_pairs={{0,4},{2,6},{4,0},{6,2},{8,12},{10,14},{12,8},{14,10},{16,20},{18,... | collective-permute-start | bytes 49160 | tf_op jit(solution)/shard_map/ppermute | solution.py:12
  16.6 1.7 %collective-permute-done.4 = bf16[8,8,128]{2,1,0:T(8,128)(2,1)S(1)} collective-permute-done((bf16[8,8,128]{2,1,0:T(8,128)(2,1)S(1)}, bf16[8,8,128]{2,1,0:T(8,128)(2,1)S(1)}, u32[]{:S(2)}, u32[]{:S(2)}) %collective-permute-start.4) | collective-permute-done | bytes 16416 | tf_op jit(solution)/shard_map/ppermute | solution.py:12
  18.4 0.6 gather_fusion.1
  18.9 1.1 fusion.94
  20.1 1.2 collective-permute-done.5
  21.2 2.0 %collective-permute-start.6 = (bf16[4,8,128]{2,1,0:T(8,128)(2,1)S(1)}, bf16[4,8,128]{2,1,0:T(8,128)(2,1)S(1)}, u32[]{:S(2)}, u32[]{:S(2)}) collective-permute-start(bf16[4,8,128]{2,1,0:T(8,128)(2,1)S(1)} %maximum_select_fusion.26), channel_id=1, source_target_pairs={{0,2},{2,0},{4,6},{6,4},{8,10},{10,8},{12,14},{14,12},{16,18},{18,... | collective-permute-start | bytes 24584 | tf_op jit(solution)/shard_map/ppermute | solution.py:12
  23.4 1.5 collective-permute-done.6
  24.9 2.0 %collective-permute-start.7 = (bf16[8,8,128]{2,1,0:T(8,128)(2,1)S(1)}, bf16[8,8,128]{2,1,0:T(8,128)(2,1)S(1)}, u32[]{:S(2)}, u32[]{:S(2)}) collective-permute-start(bf16[8,8,128]{2,1,0:T(8,128)(2,1)S(1)} %maximum_select_fusion.22), channel_id=1, source_target_pairs={{0,4},{2,6},{4,0},{6,2},{8,12},{10,14},{12,8},{14,10},{16,20},{18,... | collective-permute-start | bytes 49160 | tf_op jit(solution)/shard_map/ppermute | solution.py:12
  27.0 1.6 %collective-permute-done.7 = bf16[8,8,128]{2,1,0:T(8,128)(2,1)S(1)} collective-permute-done((bf16[8,8,128]{2,1,0:T(8,128)(2,1)S(1)}, bf16[8,8,128]{2,1,0:T(8,128)(2,1)S(1)}, u32[]{:S(2)}, u32[]{:S(2)}) %collective-permute-start.7) | collective-permute-done | bytes 16416 | tf_op jit(solution)/shard_map/ppermute | solution.py:12
  28.6 2.1 %collective-permute-start.8 = (bf16[16,8,128]{2,1,0:T(8,128)(2,1)S(1)}, bf16[16,8,128]{2,1,0:T(8,128)(2,1)S(1)}, u32[]{:S(2)}, u32[]{:S(2)}) collective-permute-start(bf16[16,8,128]{2,1,0:T(8,128)(2,1)S(1)} %maximum_select_fusion.18), channel_id=1, source_target_pairs={{0,8},{2,10},{4,12},{6,14},{8,0},{10,2},{12,4},{14,6},{16,24},{18,... | collective-permute-start | bytes 98312 | tf_op jit(solution)/shard_map/ppermute | solution.py:12
  30.8 1.9 %collective-permute-done.8 = bf16[16,8,128]{2,1,0:T(8,128)(2,1)S(1)} collective-permute-done((bf16[16,8,128]{2,1,0:T(8,128)(2,1)S(1)}, bf16[16,8,128]{2,1,0:T(8,128)(2,1)S(1)}, u32[]{:S(2)}, u32[]{:S(2)}) %collective-permute-start.8) | collective-permute-done | bytes 32800 | tf_op jit(solution)/shard_map/ppermute | solution.py:12
  32.7 0.6 gather_fusion.2
  33.5 1.2 collective-permute-done.9
  34.6 1.9 %collective-permute-start.10 = (bf16[4,8,128]{2,1,0:T(8,128)(2,1)S(1)}, bf16[4,8,128]{2,1,0:T(8,128)(2,1)S(1)}, u32[]{:S(2)}, u32[]{:S(2)}) collective-permute-start(bf16[4,8,128]{2,1,0:T(8,128)(2,1)S(1)} %maximum_select_fusion.27), channel_id=1, source_target_pairs={{0,2},{2,0},{4,6},{6,4},{8,10},{10,8},{12,14},{14,12},{16,18},{18,... | collective-permute-start | bytes 24584 | tf_op jit(solution)/shard_map/ppermute | solution.py:12
  36.6 1.7 %collective-permute-done.10 = bf16[4,8,128]{2,1,0:T(8,128)(2,1)S(1)} collective-permute-done((bf16[4,8,128]{2,1,0:T(8,128)(2,1)S(1)}, bf16[4,8,128]{2,1,0:T(8,128)(2,1)S(1)}, u32[]{:S(2)}, u32[]{:S(2)}) %collective-permute-start.10) | collective-permute-done | bytes 8224 | tf_op jit(solution)/shard_map/ppermute | solution.py:12
  38.3 2.0 %collective-permute-start.11 = (bf16[8,8,128]{2,1,0:T(8,128)(2,1)S(1)}, bf16[8,8,128]{2,1,0:T(8,128)(2,1)S(1)}, u32[]{:S(2)}, u32[]{:S(2)}) collective-permute-start(bf16[8,8,128]{2,1,0:T(8,128)(2,1)S(1)} %maximum_select_fusion.23), channel_id=1, source_target_pairs={{0,4},{2,6},{4,0},{6,2},{8,12},{10,14},{12,8},{14,10},{16,20},{18,... | collective-permute-start | bytes 49160 | tf_op jit(solution)/shard_map/ppermute | solution.py:12
  40.3 1.8 %collective-permute-done.11 = bf16[8,8,128]{2,1,0:T(8,128)(2,1)S(1)} collective-permute-done((bf16[8,8,128]{2,1,0:T(8,128)(2,1)S(1)}, bf16[8,8,128]{2,1,0:T(8,128)(2,1)S(1)}, u32[]{:S(2)}, u32[]{:S(2)}) %collective-permute-start.11) | collective-permute-done | bytes 16416 | tf_op jit(solution)/shard_map/ppermute | solution.py:12
  42.0 2.1 %collective-permute-start.12 = (bf16[16,8,128]{2,1,0:T(8,128)(2,1)S(1)}, bf16[16,8,128]{2,1,0:T(8,128)(2,1)S(1)}, u32[]{:S(2)}, u32[]{:S(2)}) collective-permute-start(bf16[16,8,128]{2,1,0:T(8,128)(2,1)S(1)} %maximum_select_fusion.19), channel_id=1, source_target_pairs={{0,8},{2,10},{4,12},{6,14},{8,0},{10,2},{12,4},{14,6},{16,24},{18,... | collective-permute-start | bytes 98312 | tf_op jit(solution)/shard_map/ppermute | solution.py:12
  44.2 1.8 %collective-permute-done.12 = bf16[16,8,128]{2,1,0:T(8,128)(2,1)S(1)} collective-permute-done((bf16[16,8,128]{2,1,0:T(8,128)(2,1)S(1)}, bf16[16,8,128]{2,1,0:T(8,128)(2,1)S(1)}, u32[]{:S(2)}, u32[]{:S(2)}) %collective-permute-start.12) | collective-permute-done | bytes 32800 | tf_op jit(solution)/shard_map/ppermute | solution.py:12
  46.0 3.4 %collective-permute-start.13 = (bf16[32,8,128]{2,1,0:T(8,128)(2,1)S(1)}, bf16[32,8,128]{2,1,0:T(8,128)(2,1)S(1)}, u32[]{:S(2)}, u32[]{:S(2)}) collective-permute-start(bf16[32,8,128]{2,1,0:T(8,128)(2,1)S(1)} %maximum_select_fusion.12), channel_id=1, source_target_pairs={{0,16},{2,18},{4,20},{6,22},{8,24},{10,26},{12,28},{14,30},{16,0},... | collective-permute-start | bytes 196616 | tf_op jit(solution)/shard_map/ppermute | solution.py:12
  49.5 2.2 %collective-permute-done.13 = bf16[32,8,128]{2,1,0:T(8,128)(2,1)S(1)} collective-permute-done((bf16[32,8,128]{2,1,0:T(8,128)(2,1)S(1)}, bf16[32,8,128]{2,1,0:T(8,128)(2,1)S(1)}, u32[]{:S(2)}, u32[]{:S(2)}) %collective-permute-start.13) | collective-permute-done | bytes 65568 | tf_op jit(solution)/shard_map/ppermute | solution.py:12
  51.7 0.6 gather_fusion.3
  52.3 0.3 convolution_multiply_fusion.4
  52.8 1.2 collective-permute-done.14
  54.0 1.5 collective-permute-start.15
  55.5 2.6 %collective-permute-done.15 = f32[4,3,8,128]{3,2,1,0:T(8,128)S(1)} collective-permute-done((f32[4,3,8,128]{3,2,1,0:T(8,128)S(1)}, f32[4,3,8,128]{3,2,1,0:T(8,128)S(1)}, u32[]{:S(2)}, u32[]{:S(2)}) %collective-permute-start.15) | collective-permute-done | bytes 49184 | tf_op jit(solution)/shard_map/ppermute | solution.py:12
  58.1 1.6 collective-permute-start.16
  59.7 3.1 %collective-permute-done.16 = f32[8,3,8,128]{3,2,1,0:T(8,128)S(1)} collective-permute-done((f32[8,3,8,128]{3,2,1,0:T(8,128)S(1)}, f32[8,3,8,128]{3,2,1,0:T(8,128)S(1)}, u32[]{:S(2)}, u32[]{:S(2)}) %collective-permute-start.16) | collective-permute-done | bytes 98336 | tf_op jit(solution)/shard_map/ppermute | solution.py:12
  62.8 1.6 %collective-permute-start.17 = (f32[16,3,8,128]{3,2,1,0:T(8,128)S(1)}, f32[16,3,8,128]{3,2,1,0:T(8,128)S(1)}, u32[]{:S(2)}, u32[]{:S(2)}) collective-permute-start(f32[16,3,8,128]{3,2,1,0:T(8,128)S(1)} %maximum_select_fusion.3), channel_id=1, source_target_pairs={{0,8},{2,10},{4,12},{6,14},{8,0},{10,2},{12,4},{14,6},{16,24},{18,... | collective-permute-start | bytes 589832 | tf_op jit(solution)/shard_map/ppermute | solution.py:12
  64.4 4.1 %collective-permute-done.17 = f32[16,3,8,128]{3,2,1,0:T(8,128)S(1)} collective-permute-done((f32[16,3,8,128]{3,2,1,0:T(8,128)S(1)}, f32[16,3,8,128]{3,2,1,0:T(8,128)S(1)}, u32[]{:S(2)}, u32[]{:S(2)}) %collective-permute-start.17) | collective-permute-done | bytes 196640 | tf_op jit(solution)/shard_map/ppermute | solution.py:12
  68.6 3.6 %collective-permute-start.18 = (f32[32,3,8,128]{3,2,1,0:T(8,128)S(1)}, f32[32,3,8,128]{3,2,1,0:T(8,128)S(1)}, u32[]{:S(2)}, u32[]{:S(2)}) collective-permute-start(f32[32,3,8,128]{3,2,1,0:T(8,128)S(1)} %maximum_select_fusion.1), channel_id=1, source_target_pairs={{0,16},{2,18},{4,20},{6,22},{8,24},{10,26},{12,28},{14,30},{16,0},... | collective-permute-start | bytes 1179656 | tf_op jit(solution)/shard_map/ppermute | solution.py:12
  72.1 0.7 copy-done.6
  73.1 13.1 %collective-permute-done.18 = f32[32,3,8,128]{3,2,1,0:T(8,128)S(1)} collective-permute-done((f32[32,3,8,128]{3,2,1,0:T(8,128)S(1)}, f32[32,3,8,128]{3,2,1,0:T(8,128)S(1)}, u32[]{:S(2)}, u32[]{:S(2)}) %collective-permute-start.18) | collective-permute-done | bytes 393248 | tf_op jit(solution)/shard_map/ppermute | solution.py:12
  86.2 0.4 fusion.11
  87.0 1.2 collective-permute-done.19
  88.2 1.5 collective-permute-start.20
  89.7 2.6 %collective-permute-done.20 = f32[4,3,8,128]{3,2,1,0:T(8,128)S(1)} collective-permute-done((f32[4,3,8,128]{3,2,1,0:T(8,128)S(1)}, f32[4,3,8,128]{3,2,1,0:T(8,128)S(1)}, u32[]{:S(2)}, u32[]{:S(2)}) %collective-permute-start.20) | collective-permute-done | bytes 49184 | tf_op jit(solution)/shard_map/ppermute | solution.py:12
  92.3 1.6 collective-permute-start.21
  93.9 3.1 %collective-permute-done.21 = f32[8,3,8,128]{3,2,1,0:T(8,128)S(1)} collective-permute-done((f32[8,3,8,128]{3,2,1,0:T(8,128)S(1)}, f32[8,3,8,128]{3,2,1,0:T(8,128)S(1)}, u32[]{:S(2)}, u32[]{:S(2)}) %collective-permute-start.21) | collective-permute-done | bytes 98336 | tf_op jit(solution)/shard_map/ppermute | solution.py:12
  97.0 0.8 collective-permute-start.22
  98.1 4.7 %collective-permute-done.22 = f32[16,3,8,128]{3,2,1,0:T(8,128)S(1)} collective-permute-done((f32[16,3,8,128]{3,2,1,0:T(8,128)S(1)}, f32[16,3,8,128]{3,2,1,0:T(8,128)S(1)}, u32[]{:S(2)}, u32[]{:S(2)}) %collective-permute-start.22) | collective-permute-done | bytes 196640 | tf_op jit(solution)/shard_map/ppermute | solution.py:12
  102.8 0.3 fusion.14
  103.4 1.2 collective-permute-done.23
  104.6 1.5 collective-permute-start.24
  106.4 2.3 %collective-permute-done.24 = f32[4,3,8,128]{3,2,1,0:T(8,128)S(1)} collective-permute-done((f32[4,3,8,128]{3,2,1,0:T(8,128)S(1)}, f32[4,3,8,128]{3,2,1,0:T(8,128)S(1)}, u32[]{:S(2)}, u32[]{:S(2)}) %collective-permute-start.24) | collective-permute-done | bytes 49184 | tf_op jit(solution)/shard_map/ppermute | solution.py:12
  108.7 1.6 collective-permute-start.25
  110.3 3.1 %collective-permute-done.25 = f32[8,3,8,128]{3,2,1,0:T(8,128)S(1)} collective-permute-done((f32[8,3,8,128]{3,2,1,0:T(8,128)S(1)}, f32[8,3,8,128]{3,2,1,0:T(8,128)S(1)}, u32[]{:S(2)}, u32[]{:S(2)}) %collective-permute-start.25) | collective-permute-done | bytes 98336 | tf_op jit(solution)/shard_map/ppermute | solution.py:12
  114.0 1.1 collective-permute-done.26
  115.2 1.5 collective-permute-start.27
  116.8 2.4 %collective-permute-done.27 = f32[4,3,8,128]{3,2,1,0:T(8,128)S(1)} collective-permute-done((f32[4,3,8,128]{3,2,1,0:T(8,128)S(1)}, f32[4,3,8,128]{3,2,1,0:T(8,128)S(1)}, u32[]{:S(2)}, u32[]{:S(2)}) %collective-permute-start.27) | collective-permute-done | bytes 49184 | tf_op jit(solution)/shard_map/ppermute | solution.py:12
  119.8 0.9 fusion.17
  120.7 40.0 %all-reduce = (f32[8]{0:T(128)S(1)}, f32[8,8]{0,1:T(8,128)S(1)}) all-reduce(f32[8]{0:T(128)S(1)} %multiply_reduce_fusion, f32[8,8]{0,1:T(8,128)S(1)} %bitcast.256), channel_id=1, replica_groups=mesh['leaf'=16,'tile'=2] {'leaf','tile'}, use_global_device_ids=true, to_apply=%region_2.3 | all-reduce | flops 72 | bytes 576 | tf_op jit(solution)/shard_map/psum | solution.py:94
  160.9 0.7 pad_maximum_fusion
  (101 shorter events, 4.5 us)
Async XLA Ops:
  0.6 119.2 %copy-start = (f32[8,5,2,8,128]{4,3,2,1,0:T(8,128)S(1)}, f32[8,5,2,8,128]{4,3,2,1,0:T(8,128)}, u32[]{:S(2)}) copy-start(f32[8,5,2,8,128]{4,3,2,1,0:T(8,128)} %param.13) | copy-start | bytes 983044
  0.6 0.7 copy-start.7
  0.7 32.6 %copy-start.1 = (bf16[4,2,3,128,128]{4,3,2,1,0:T(8,128)(2,1)S(1)}, bf16[4,2,3,128,128]{4,3,2,1,0:T(8,128)(2,1)}, u32[]{:S(2)}) copy-start(bf16[4,2,3,128,128]{4,3,2,1,0:T(8,128)(2,1)} %param.8) | copy-start | bytes 2359300
  2.2 1.7 %collective-permute-start = (bf16[2,8,128]{2,1,0:T(8,128)(2,1)S(1)}, bf16[2,8,128]{2,1,0:T(8,128)(2,1)S(1)}, u32[]{:S(2)}, u32[]{:S(2)}) collective-permute-start(bf16[2,8,128]{2,1,0:T(8,128)(2,1)S(1)} %fusion.60), channel_id=1, source_target_pairs={{0,1},{1,0},{2,3},{3,2},{4,5},{5,4},{6,7},{7,6},{8,9},{9,8},{10,11... | collective-permute-start | bytes 12296 | tf_op jit(solution)/shard_map/ppermute | solution.py:12
  3.9 4.2 %collective-permute-start.1 = (bf16[4,8,128]{2,1,0:T(8,128)(2,1)S(1)}, bf16[4,8,128]{2,1,0:T(8,128)(2,1)S(1)}, u32[]{:S(2)}, u32[]{:S(2)}) collective-permute-start(bf16[4,8,128]{2,1,0:T(8,128)(2,1)S(1)} %maximum_select_fusion.24), channel_id=1, source_target_pairs={{0,2},{2,0},{4,6},{6,4},{8,10},{10,8},{12,14},{14,12},{16,18},{18,... | collective-permute-start | bytes 24584 | tf_op jit(solution)/shard_map/ppermute | solution.py:12
  9.7 1.2 collective-permute-start.2
  10.9 3.7 %collective-permute-start.3 = (bf16[4,8,128]{2,1,0:T(8,128)(2,1)S(1)}, bf16[4,8,128]{2,1,0:T(8,128)(2,1)S(1)}, u32[]{:S(2)}, u32[]{:S(2)}) collective-permute-start(bf16[4,8,128]{2,1,0:T(8,128)(2,1)S(1)} %maximum_select_fusion.25), channel_id=1, source_target_pairs={{0,2},{2,0},{4,6},{6,4},{8,10},{10,8},{12,14},{14,12},{16,18},{18,... | collective-permute-start | bytes 24584 | tf_op jit(solution)/shard_map/ppermute | solution.py:12
  14.6 3.8 %collective-permute-start.4 = (bf16[8,8,128]{2,1,0:T(8,128)(2,1)S(1)}, bf16[8,8,128]{2,1,0:T(8,128)(2,1)S(1)}, u32[]{:S(2)}, u32[]{:S(2)}) collective-permute-start(bf16[8,8,128]{2,1,0:T(8,128)(2,1)S(1)} %maximum_select_fusion.21), channel_id=1, source_target_pairs={{0,4},{2,6},{4,0},{6,2},{8,12},{10,14},{12,8},{14,10},{16,20},{18,... | collective-permute-start | bytes 49160 | tf_op jit(solution)/shard_map/ppermute | solution.py:12
  18.9 14.3 %copy-start.5 = (f32[5,2,8,128]{3,2,1,0:T(8,128)S(1)}, f32[5,2,8,128]{3,2,1,0:T(8,128)}, u32[]{:S(2)}) copy-start(f32[5,2,8,128]{3,2,1,0:T(8,128)} %param.7) | copy-start | bytes 122884
  20.0 32.5 %copy-start.2 = (bf16[4,2,3,128,128]{4,3,2,1,0:T(8,128)(2,1)S(1)}, bf16[4,2,3,128,128]{4,3,2,1,0:T(8,128)(2,1)}, u32[]{:S(2)}) copy-start(bf16[4,2,3,128,128]{4,3,2,1,0:T(8,128)(2,1)} %param.9) | copy-start | bytes 2359300
  20.0 1.2 collective-permute-start.5
  21.2 3.7 %collective-permute-start.6 = (bf16[4,8,128]{2,1,0:T(8,128)(2,1)S(1)}, bf16[4,8,128]{2,1,0:T(8,128)(2,1)S(1)}, u32[]{:S(2)}, u32[]{:S(2)}) collective-permute-start(bf16[4,8,128]{2,1,0:T(8,128)(2,1)S(1)} %maximum_select_fusion.26), channel_id=1, source_target_pairs={{0,2},{2,0},{4,6},{6,4},{8,10},{10,8},{12,14},{14,12},{16,18},{18,... | collective-permute-start | bytes 24584 | tf_op jit(solution)/shard_map/ppermute | solution.py:12
  24.9 3.7 %collective-permute-start.7 = (bf16[8,8,128]{2,1,0:T(8,128)(2,1)S(1)}, bf16[8,8,128]{2,1,0:T(8,128)(2,1)S(1)}, u32[]{:S(2)}, u32[]{:S(2)}) collective-permute-start(bf16[8,8,128]{2,1,0:T(8,128)(2,1)S(1)} %maximum_select_fusion.22), channel_id=1, source_target_pairs={{0,4},{2,6},{4,0},{6,2},{8,12},{10,14},{12,8},{14,10},{16,20},{18,... | collective-permute-start | bytes 49160 | tf_op jit(solution)/shard_map/ppermute | solution.py:12
  28.6 4.0 %collective-permute-start.8 = (bf16[16,8,128]{2,1,0:T(8,128)(2,1)S(1)}, bf16[16,8,128]{2,1,0:T(8,128)(2,1)S(1)}, u32[]{:S(2)}, u32[]{:S(2)}) collective-permute-start(bf16[16,8,128]{2,1,0:T(8,128)(2,1)S(1)} %maximum_select_fusion.18), channel_id=1, source_target_pairs={{0,8},{2,10},{4,12},{6,14},{8,0},{10,2},{12,4},{14,6},{16,24},{18,... | collective-permute-start | bytes 98312 | tf_op jit(solution)/shard_map/ppermute | solution.py:12
  33.4 18.9 %copy-start.3 = (bf16[5,2,128,128]{3,2,1,0:T(8,128)(2,1)S(1)}, bf16[5,2,128,128]{3,2,1,0:T(8,128)(2,1)}, u32[]{:S(2)}) copy-start(bf16[5,2,128,128]{3,2,1,0:T(8,128)(2,1)} %param.10) | copy-start | bytes 983044
  33.4 1.2 collective-permute-start.9
  34.6 3.7 %collective-permute-start.10 = (bf16[4,8,128]{2,1,0:T(8,128)(2,1)S(1)}, bf16[4,8,128]{2,1,0:T(8,128)(2,1)S(1)}, u32[]{:S(2)}, u32[]{:S(2)}) collective-permute-start(bf16[4,8,128]{2,1,0:T(8,128)(2,1)S(1)} %maximum_select_fusion.27), channel_id=1, source_target_pairs={{0,2},{2,0},{4,6},{6,4},{8,10},{10,8},{12,14},{14,12},{16,18},{18,... | collective-permute-start | bytes 24584 | tf_op jit(solution)/shard_map/ppermute | solution.py:12
  38.3 3.7 %collective-permute-start.11 = (bf16[8,8,128]{2,1,0:T(8,128)(2,1)S(1)}, bf16[8,8,128]{2,1,0:T(8,128)(2,1)S(1)}, u32[]{:S(2)}, u32[]{:S(2)}) collective-permute-start(bf16[8,8,128]{2,1,0:T(8,128)(2,1)S(1)} %maximum_select_fusion.23), channel_id=1, source_target_pairs={{0,4},{2,6},{4,0},{6,2},{8,12},{10,14},{12,8},{14,10},{16,20},{18,... | collective-permute-start | bytes 49160 | tf_op jit(solution)/shard_map/ppermute | solution.py:12
  42.0 4.0 %collective-permute-start.12 = (bf16[16,8,128]{2,1,0:T(8,128)(2,1)S(1)}, bf16[16,8,128]{2,1,0:T(8,128)(2,1)S(1)}, u32[]{:S(2)}, u32[]{:S(2)}) collective-permute-start(bf16[16,8,128]{2,1,0:T(8,128)(2,1)S(1)} %maximum_select_fusion.19), channel_id=1, source_target_pairs={{0,8},{2,10},{4,12},{6,14},{8,0},{10,2},{12,4},{14,6},{16,24},{18,... | collective-permute-start | bytes 98312 | tf_op jit(solution)/shard_map/ppermute | solution.py:12
  46.0 5.7 %collective-permute-start.13 = (bf16[32,8,128]{2,1,0:T(8,128)(2,1)S(1)}, bf16[32,8,128]{2,1,0:T(8,128)(2,1)S(1)}, u32[]{:S(2)}, u32[]{:S(2)}) collective-permute-start(bf16[32,8,128]{2,1,0:T(8,128)(2,1)S(1)} %maximum_select_fusion.12), channel_id=1, source_target_pairs={{0,16},{2,18},{4,20},{6,22},{8,24},{10,26},{12,28},{14,30},{16,0},... | collective-permute-start | bytes 196616 | tf_op jit(solution)/shard_map/ppermute | solution.py:12
  52.8 1.2 collective-permute-start.14
  54.0 4.1 %collective-permute-start.15 = (f32[4,3,8,128]{3,2,1,0:T(8,128)S(1)}, f32[4,3,8,128]{3,2,1,0:T(8,128)S(1)}, u32[]{:S(2)}, u32[]{:S(2)}) collective-permute-start(f32[4,3,8,128]{3,2,1,0:T(8,128)S(1)} %maximum_select_fusion.13), channel_id=1, source_target_pairs={{0,2},{2,0},{4,6},{6,4},{8,10},{10,8},{12,14},{14,12},{16,18},{18,... | collective-permute-start | bytes 147464 | tf_op jit(solution)/shard_map/ppermute | solution.py:12
  58.1 4.7 %collective-permute-start.16 = (f32[8,3,8,128]{3,2,1,0:T(8,128)S(1)}, f32[8,3,8,128]{3,2,1,0:T(8,128)S(1)}, u32[]{:S(2)}, u32[]{:S(2)}) collective-permute-start(f32[8,3,8,128]{3,2,1,0:T(8,128)S(1)} %maximum_select_fusion.7), channel_id=1, source_target_pairs={{0,4},{2,6},{4,0},{6,2},{8,12},{10,14},{12,8},{14,10},{16,20},{18,... | collective-permute-start | bytes 294920 | tf_op jit(solution)/shard_map/ppermute | solution.py:12
  62.8 5.7 %collective-permute-start.17 = (f32[16,3,8,128]{3,2,1,0:T(8,128)S(1)}, f32[16,3,8,128]{3,2,1,0:T(8,128)S(1)}, u32[]{:S(2)}, u32[]{:S(2)}) collective-permute-start(f32[16,3,8,128]{3,2,1,0:T(8,128)S(1)} %maximum_select_fusion.3), channel_id=1, source_target_pairs={{0,8},{2,10},{4,12},{6,14},{8,0},{10,2},{12,4},{14,6},{16,24},{18,... | collective-permute-start | bytes 589832 | tf_op jit(solution)/shard_map/ppermute | solution.py:12
  68.6 17.6 %collective-permute-start.18 = (f32[32,3,8,128]{3,2,1,0:T(8,128)S(1)}, f32[32,3,8,128]{3,2,1,0:T(8,128)S(1)}, u32[]{:S(2)}, u32[]{:S(2)}) collective-permute-start(f32[32,3,8,128]{3,2,1,0:T(8,128)S(1)} %maximum_select_fusion.1), channel_id=1, source_target_pairs={{0,16},{2,18},{4,20},{6,22},{8,24},{10,26},{12,28},{14,30},{16,0},... | collective-permute-start | bytes 1179656 | tf_op jit(solution)/shard_map/ppermute | solution.py:12
  72.1 0.7 copy-start.6
  87.0 1.2 collective-permute-start.19
  88.2 4.1 %collective-permute-start.20 = (f32[4,3,8,128]{3,2,1,0:T(8,128)S(1)}, f32[4,3,8,128]{3,2,1,0:T(8,128)S(1)}, u32[]{:S(2)}, u32[]{:S(2)}) collective-permute-start(f32[4,3,8,128]{3,2,1,0:T(8,128)S(1)} %maximum_select_fusion.14), channel_id=1, source_target_pairs={{0,2},{2,0},{4,6},{6,4},{8,10},{10,8},{12,14},{14,12},{16,18},{18,... | collective-permute-start | bytes 147464 | tf_op jit(solution)/shard_map/ppermute | solution.py:12
  92.3 4.7 %collective-permute-start.21 = (f32[8,3,8,128]{3,2,1,0:T(8,128)S(1)}, f32[8,3,8,128]{3,2,1,0:T(8,128)S(1)}, u32[]{:S(2)}, u32[]{:S(2)}) collective-permute-start(f32[8,3,8,128]{3,2,1,0:T(8,128)S(1)} %maximum_select_fusion.8), channel_id=1, source_target_pairs={{0,4},{2,6},{4,0},{6,2},{8,12},{10,14},{12,8},{14,10},{16,20},{18,... | collective-permute-start | bytes 294920 | tf_op jit(solution)/shard_map/ppermute | solution.py:12
  97.0 5.7 %collective-permute-start.22 = (f32[16,3,8,128]{3,2,1,0:T(8,128)S(1)}, f32[16,3,8,128]{3,2,1,0:T(8,128)S(1)}, u32[]{:S(2)}, u32[]{:S(2)}) collective-permute-start(f32[16,3,8,128]{3,2,1,0:T(8,128)S(1)} %maximum_select_fusion.4), channel_id=1, source_target_pairs={{0,8},{2,10},{4,12},{6,14},{8,0},{10,2},{12,4},{14,6},{16,24},{18,... | collective-permute-start | bytes 589832 | tf_op jit(solution)/shard_map/ppermute | solution.py:12
  103.4 1.2 collective-permute-start.23
  104.6 4.1 %collective-permute-start.24 = (f32[4,3,8,128]{3,2,1,0:T(8,128)S(1)}, f32[4,3,8,128]{3,2,1,0:T(8,128)S(1)}, u32[]{:S(2)}, u32[]{:S(2)}) collective-permute-start(f32[4,3,8,128]{3,2,1,0:T(8,128)S(1)} %maximum_select_fusion.15), channel_id=1, source_target_pairs={{0,2},{2,0},{4,6},{6,4},{8,10},{10,8},{12,14},{14,12},{16,18},{18,... | collective-permute-start | bytes 147464 | tf_op jit(solution)/shard_map/ppermute | solution.py:12
  108.7 4.7 %collective-permute-start.25 = (f32[8,3,8,128]{3,2,1,0:T(8,128)S(1)}, f32[8,3,8,128]{3,2,1,0:T(8,128)S(1)}, u32[]{:S(2)}, u32[]{:S(2)}) collective-permute-start(f32[8,3,8,128]{3,2,1,0:T(8,128)S(1)} %maximum_select_fusion.9), channel_id=1, source_target_pairs={{0,4},{2,6},{4,0},{6,2},{8,12},{10,14},{12,8},{14,10},{16,20},{18,... | collective-permute-start | bytes 294920 | tf_op jit(solution)/shard_map/ppermute | solution.py:12
  113.9 1.2 collective-permute-start.26
  115.2 4.1 %collective-permute-start.27 = (f32[4,3,8,128]{3,2,1,0:T(8,128)S(1)}, f32[4,3,8,128]{3,2,1,0:T(8,128)S(1)}, u32[]{:S(2)}, u32[]{:S(2)}) collective-permute-start(f32[4,3,8,128]{3,2,1,0:T(8,128)S(1)} %maximum_select_fusion.16), channel_id=1, source_target_pairs={{0,2},{2,0},{4,6},{6,4},{8,10},{10,8},{12,14},{14,12},{16,18},{18,... | collective-permute-start | bytes 147464 | tf_op jit(solution)/shard_map/ppermute | solution.py:12
  119.7 1.1 copy-start.4
where the time goes:
time: 162 us
  waiting for transfers between devices  66.8 us (41%)
  blocking collectives  40 us (25%)
  starting transfers between devices  39.4 us (24%)
  local copies, waits for them, and re-layouts  6.37 us (4%)
  matrix products  6 us (4%)
  other arithmetic  2.14 us (1%)
    ppermute x28, waiting for transfers between devices, partner_2(): lax.ppermute(shard, axis, [(i, i ^ 1 << bit) for i in range(lax.axis_size...  66.8 us
    psum x1, blocking collectives, local(): lax.psum((local_proj, jnp.sum(precond * precond, axis=(0, 1, 3))), ('leaf...  40 us
    ppermute x28, starting transfers between devices, partner_2(): lax.ppermute(shard, axis, [(i, i ^ 1 << bit) for i in range(lax.axis_size...  39.4 us
  transfers between devices with their start and end apart: 28, of which 27 were waited for; matrix products, arithmetic and copies ran while one was open for 2% of the time, Pallas kernels for 0%

commit v1 on v0

v1 whole, which is shorter than its diff:
```python
import functools
import math

import jax
import jax.numpy as jnp
from jax import lax
from jax.experimental import pallas as pl
from jax.experimental.pallas import tpu as pltpu
from jax.sharding import PartitionSpec as P

epsilon = 1e-06
MESH = pl.DeviceIdType.MESH
NT = (((1,), (1,)), ((), ()))


def split(index, size):
    if size & (size - 1) == 0:
        return lax.shift_right_logical(index, size.bit_length() - 1), index & (size - 1)
    return index // size, index % size


def kernel(dims, *refs):
    levels, tiles, columns, rows, neighbours, basis_size, n_leaf, n_tile = dims
    devices = n_leaf * n_tile
    width = tiles * columns
    pairs = tiles * neighbours
    refs = list(refs)

    def take(count):
        taken = refs[:count]
        del refs[:count]
        return taken

    rhs_any, lower_any, upper_any, diag_any, pattern_any, counts_any, basis_any = take(7)
    precond_ref, coeffs_ref = take(2)
    rhs_v, lower_v, upper_v, diag_v, pattern_v, counts_v, basis_v = take(7)
    gathered = take(levels - 1)
    outgoing = take(levels - 1)
    incoming = take(levels - 1)
    pick = take(levels - 1)
    spread = take(levels - 1)
    (totals,) = take(1)
    load_sem, fwd_send, fwd_recv, bwd_send, bwd_recv, sum_send, sum_recv = take(7)

    leaf = lax.axis_index("leaf")
    tile = lax.axis_index("tile")
    me = leaf * n_tile + tile

    def load(number, source, target):
        copy = pltpu.make_async_copy(source, target, load_sem.at[number])
        copy.start()
        return copy

    rhs_load = load(0, rhs_any, rhs_v)
    pattern_load = load(1, pattern_any, pattern_v)
    counts_load = load(2, counts_any, counts_v)
    lower_load = [
        load(3 + k, lower_any.at[k], lower_v.at[k]) for k in range(levels - 1)
    ]
    diag_load = load(levels + 2, diag_any, diag_v)
    upper_load = load(levels + 3, upper_any, upper_v)
    basis_load = load(levels + 4, basis_any, basis_v)

    def each_peer(leaves, visit):
        first = lax.div(leaf, leaves) * leaves
        own = leaf - first
        others = [(tile + step) % n_tile if step else tile for step in range(n_tile)]

        def far(step, carry):
            near = lax.rem(own + step, leaves)
            for other in others:
                visit(first + near, other, near * n_tile + other)
            return carry

        if leaves <= 16:
            for step in range(leaves // 2, leaves):
                far(step, 0)
            for step in range(1, leaves // 2):
                far(step, 0)
        else:
            lax.fori_loop(1, leaves, far, 0)
        for other in others[1:]:
            visit(leaf, other, own * n_tile + other)

    barrier = pltpu.get_barrier_semaphore()

    def greet(to_leaf, to_tile, index):
        pl.semaphore_signal(barrier, inc=1, device_id=(to_leaf, to_tile), device_id_type=MESH)

    each_peer(n_leaf, greet)

    rhs_load.wait()
    pattern_load.wait()
    counts_load.wait()
    live = [
        [
            (counts_v[k : k + 1, 0:1] > t).astype(jnp.float32)
            for t in range(tiles)
        ]
        for k in range(levels)
    ]

    def selectors(k):
        span = gathered[k].shape[0]
        table = pattern_v[k]
        row = lax.broadcasted_iota(jnp.int32, table.shape, 0)
        numbers = []
        for t in range(tiles):
            mine = jnp.sum(
                jnp.where(row == me * tiles + t, table, 0), axis=0, keepdims=True
            )
            numbers += [mine[:, n : n + 1] for n in range(neighbours)]
        lane_tile, lane_column = split(
            lax.broadcasted_iota(jnp.int32, (columns, span * width), 1), columns
        )
        same = lane_column == lax.broadcasted_iota(jnp.int32, (columns, span * width), 0)
        blocks = [
            jnp.where(same & (lane_tile == number), 1.0, 0.0) for number in numbers
        ]
        pick[k][...] = jnp.concatenate(blocks, 0).astype(jnp.bfloat16)
        lane_pair, lane_column = split(
            lax.broadcasted_iota(jnp.int32, (1, pairs * columns), 1), columns
        )
        wanted = jnp.zeros((1, pairs * columns), jnp.int32)
        for q, number in enumerate(numbers):
            wanted = jnp.where(lane_pair == q, number, wanted)
        row_tile, row_column = split(
            lax.broadcasted_iota(jnp.int32, (span * width, pairs * columns), 0), columns
        )
        chosen = (row_tile == wanted) & (row_column == lane_column)
        spread[k][...] = jnp.where(chosen, 1.0, 0.0).astype(jnp.bfloat16)

    selectors(0)

    def group(k):
        span = gathered[k].shape[0]
        return span, lax.rem(me, span)

    def arrived(buffer, semaphore, span):
        part = buffer.at[pl.ds(0, span - 1)]
        pltpu.make_async_copy(part, part, semaphore).wait()

    forward_vals = [[live[0][t] * rhs_v[0, t] for t in range(tiles)]]
    for k in range(1, levels):
        buffer = gathered[k - 1]
        span, slot = group(k - 1)
        buffer[slot] = jnp.concatenate(forward_vals[-1], 0).astype(jnp.bfloat16)
        if k == 1:
            pl.semaphore_wait(barrier, devices - 1)

        def send(to_leaf, to_tile, index):
            pltpu.make_async_remote_copy(
                src_ref=buffer.at[slot],
                dst_ref=buffer.at[slot],
                send_sem=fwd_send.at[k - 1],
                recv_sem=fwd_recv.at[k - 1],
                device_id=(to_leaf, to_tile),
                device_id_type=MESH,
            ).start()

        each_peer(span // n_tile, send)
        if k < levels - 1:
            selectors(k)
        lower_load[k - 1].wait()
        arrived(buffer, fwd_recv.at[k - 1], span)
        picked = jnp.dot(
            pick[k - 1][...],
            buffer[...].reshape(span * width, rows),
            preferred_element_type=jnp.float32,
        ).astype(jnp.bfloat16)
        values = []
        for t in range(tiles):
            coupling = None
            for n in range(neighbours):
                q = t * neighbours + n
                term = lax.dot_general(
                    picked[q * columns : (q + 1) * columns],
                    lower_v[k - 1, t, n],
                    NT,
                    preferred_element_type=jnp.float32,
                )
                coupling = term if coupling is None else coupling + term
            values.append(live[k][t] * (rhs_v[k, t] - coupling))
        forward_vals.append(values)

    diag_load.wait()
    upper_load.wait()
    basis_load.wait()
    partial = [None] * basis_size
    squares = None

    def project(k, values):
        nonlocal squares
        for t in range(tiles):
            for m in range(basis_size):
                term = basis_v[m, k, t] * values[t]
                partial[m] = term if partial[m] is None else partial[m] + term
            term = values[t] * values[t]
            squares = term if squares is None else squares + term

    upstream = None
    for k in reversed(range(levels)):
        values = []
        for t in range(tiles):
            operand = forward_vals[k][t]
            if upstream is not None:
                operand = operand - upstream[t * columns : (t + 1) * columns]
            value = live[k][t] * lax.dot_general(
                operand.astype(jnp.bfloat16),
                diag_v[k, t],
                NT,
                preferred_element_type=jnp.float32,
            )
            precond_ref[k, t] = value
            values.append(value)
        if k > 0:
            span, slot = group(k - 1)
            products = []
            for t in range(tiles):
                rounded = values[t].astype(jnp.bfloat16)
                for n in range(neighbours):
                    products.append(
                        lax.dot_general(
                            rounded,
                            upper_v[k - 1, t, n],
                            NT,
                            preferred_element_type=jnp.float32,
                        )
                    )
            products = jnp.concatenate(products, 0).astype(jnp.bfloat16)
            out, into = outgoing[k - 1], incoming[k - 1]
            out[...] = (
                jnp.dot(spread[k - 1][...], products, preferred_element_type=jnp.float32)
                .astype(jnp.bfloat16)
                .reshape(span, width, rows)
            )

            def send(to_leaf, to_tile, index):
                pltpu.make_async_remote_copy(
                    src_ref=out.at[index],
                    dst_ref=into.at[slot],
                    send_sem=bwd_send.at[k - 1],
                    recv_sem=bwd_recv.at[k - 1],
                    device_id=(to_leaf, to_tile),
                    device_id_type=MESH,
                ).start()

            each_peer(span // n_tile, send)
            into[slot] = out[slot]
            project(k, values)
            arrived(into, bwd_recv.at[k - 1], span)
            upstream = jnp.sum(into[...].astype(jnp.float32), axis=0)
        else:
            project(k, values)

    lane = lax.broadcasted_iota(jnp.int32, (columns, rows), 1)
    packed = jnp.zeros((columns, rows), jnp.float32)
    for m, term in enumerate(partial + [squares]):
        packed = jnp.where(lane == m, jnp.sum(term, axis=1, keepdims=True), packed)
    totals[me] = packed

    def send(to_leaf, to_tile, index):
        pltpu.make_async_remote_copy(
            src_ref=totals.at[me],
            dst_ref=totals.at[me],
            send_sem=sum_send,
            recv_sem=sum_recv,
            device_id=(to_leaf, to_tile),
            device_id_type=MESH,
        ).start()

    each_peer(n_leaf, send)
    for k in range(1, levels):
        span, slot = group(k - 1)
        arrived(gathered[k - 1], fwd_send.at[k - 1], span)
        arrived(outgoing[k - 1], bwd_send.at[k - 1], span)
    arrived(totals, sum_recv, devices)
    total = jnp.sum(totals[...], axis=0)
    squared = jnp.sum(jnp.where(lane == basis_size, total, 0.0), axis=1, keepdims=True)
    explained = jnp.sum(
        jnp.where(lane < basis_size, total * total, 0.0), axis=1, keepdims=True
    )
    norm = jnp.sqrt(jnp.maximum(squared - explained, 0.0) + epsilon)
    scaled = norm / math.sqrt(levels * tiles * rows * devices)
    result = jnp.where(lane == basis_size, scaled, total)
    coeffs_ref[...] = jnp.transpose(result)[: basis_size + 1]
    arrived(totals, sum_send, devices)


def local(rhs, lower, upper, diag_inv, pattern, counts, basis):
    levels, tiles, columns, rows = rhs.shape
    neighbours = lower.shape[2]
    basis_size = basis.shape[0]
    n_leaf, n_tile = lax.axis_size("leaf"), lax.axis_size("tile")
    dims = (levels, tiles, columns, rows, neighbours, basis_size, n_leaf, n_tile)
    spans = [2 ** (k + 1) for k in range(1, levels)]
    width, pairs = tiles * columns, tiles * neighbours
    operands = (rhs, lower, upper, diag_inv, pattern, counts, basis)
    slots = [pltpu.VMEM((span, width, rows), jnp.bfloat16) for span in spans]
    scratch = [pltpu.VMEM(operand.shape, operand.dtype) for operand in operands]
    scratch += slots * 3
    scratch += [pltpu.VMEM((pairs * columns, span * width), jnp.bfloat16) for span in spans]
    scratch += [pltpu.VMEM((span * width, pairs * columns), jnp.bfloat16) for span in spans]
    scratch += [pltpu.VMEM((n_leaf * n_tile, columns, rows), jnp.float32)]
    scratch += [pltpu.SemaphoreType.DMA((levels + 5,))]
    scratch += [pltpu.SemaphoreType.DMA((levels - 1,))] * 4
    scratch += [pltpu.SemaphoreType.DMA] * 2
    return pl.pallas_call(
        functools.partial(kernel, dims),
        name="sweep",
        out_shape=(
            jax.ShapeDtypeStruct(rhs.shape, jnp.float32),
            jax.ShapeDtypeStruct((basis_size + 1, columns), jnp.float32),
        ),
        in_specs=[pl.BlockSpec(memory_space=pl.ANY)] * len(operands),
        out_specs=[pl.BlockSpec(memory_space=pltpu.VMEM)] * 2,
        scratch_shapes=scratch,
        compiler_params=pltpu.CompilerParams(collective_id=0, has_side_effects=True),
    )(*operands)


def solution(mesh):
    return jax.shard_map(
        local,
        mesh=mesh,
        in_specs=(
            P(None, ("leaf", "tile"), None, None),
            P(None, ("leaf", "tile"), None, None, None),
            P(None, ("leaf", "tile"), None, None, None),
            P(None, ("leaf", "tile"), None, None),
            P(),
            P(None, ("leaf", "tile")),
            P(None, None, ("leaf", "tile"), None, None),
        ),
        out_specs=(P(None, ("leaf", "tile"), None, None), P()),
        check_vma=False,
    )
```

time: 162 us -> 52.4 us (0.32)
  waiting for transfers between devices: 66.8 us -> 0 us
  Pallas kernels: 0 us -> 45.9 us
  blocking collectives: 40 us -> 0 us
  starting transfers between devices: 39.4 us -> 0 us
  matrix products: 6 us -> 0 us
  other arithmetic: 2.14 us -> 0 us
    ppermute x28 -> x0, waiting for transfers between devices: 66.8 us -> none  [partner_2(): lax.ppermute(shard, axis, [(i, i ^ 1 << bit) for i in range(lax.axis_size...]
    pallas_call x0 -> x1, Pallas kernels: none -> 45.9 us  [local(): pl.pallas_call(functools.partial(kernel, dims), name='sweep', out_shape=(...]
    psum x1 -> x0, blocking collectives: 40 us -> none  [local(): lax.psum((local_proj, jnp.sum(precond * precond, axis=(0, 1, 3))), ('leaf...]
    ppermute x28 -> x0, starting transfers between devices: 39.4 us -> none  [partner_2(): lax.ppermute(shard, axis, [(i, i ^ 1 << bit) for i in range(lax.axis_size...]
    dot_general x17 -> x0, matrix products: 6 us -> none  [the longest x3 2.36 us: local(): jnp.einsum('tnab,tnrb->tra', lower[level_index - 1], picked, preferred_el...]
    unnamed x19 -> x3, local copies, waits for them, and re-layouts: 1.41 us -> 4.18 us
    gather x4 -> x0, local copies, waits for them, and re-layouts: 2.25 us -> none  [local(): picked = grouped[own_pattern[level_index - 1]]]
  transfers between devices with their start and end apart: 28 -> 0, of which waited for: 27 -> 0; matrix products, arithmetic and copies ran while one was open for 2% -> 0% of each run, Pallas kernels for 0% -> 0%
where the time goes in v1:
time: 52.4 us; the launch traced here: 52.1 us
  Pallas kernels  45.9 us (88%)
  local copies, waits for them, and re-layouts  5.55 us (11%)
  between operations  0.64 us (1%)
    pallas_call x1, Pallas kernels, local(): pl.pallas_call(functools.partial(kernel, dims), name='sweep', out_shape=(...  45.9 us
    unnamed x3, local copies, waits for them, and re-layouts  4.18 us
    pallas_call x1, local copies, waits for them, and re-layouts, local(): pl.pallas_call(functools.partial(kernel, dims), name='sweep', out_shape=(...  1.36 us

profile of v1, /device:TPU:0, one launch (start us, length us, event | category | flops | bytes accessed | tf_op | source)
XLA Modules:
  0.0 52.1 jit_solution(1392009572245370433)
XLA Ops:
  0.6 1.3 %copy.10.refs_5_ = s32[5,1]{1,0:T(8,128)} copy(s32[5,1]{0,1:T(1,128)} %param.12) | data formatting | bytes 40 | tf_op args[5]
  2.0 1.5 %copy.9.refs_4_ = s32[4,64,3]{2,1,0:T(8,128)} copy(s32[4,64,3]{1,0,2:T(4,128)} %param.11) | data formatting | bytes 6144 | tf_op args[4]
  3.4 45.9 %sweep.1 = (f32[5,2,8,128]{3,2,1,0:T(8,128)}, f32[9,8]{1,0:T(8,128)}) custom-call(f32[5,2,8,128]{3,2,1,0:T(8,128)} %refs_0_.1, bf16[4,2,3,128,128]{4,3,2,1,0:T(8,128)(2,1)} %refs_1_.1, bf16[4,2,3,128,128]{4,3,2,1,0:T(8,128)(2,1)} %refs_2_.1, bf16[5,2,128,128]{3,2,1,0:T(8,128)(2,1)} %refs_3_.1, s32[4,64,3]{2,1,0:T(8,128)} %copy.9.refs_4_, ...), custom_call_target="tpu_custom_call" | custom-call | tf_op jit(solution)/shard_map/sweep/pallas_call | solution.py:308
  49.4 1.4 %copy.11 = f32[9,8]{0,1:T(8,128)} copy(f32[9,8]{1,0:T(8,128)} %get-tuple-element.3) | data formatting | bytes 576 | tf_op jit(solution)/shard_map/sweep/pallas_call | solution.py:308
  50.7 1.4 %copy.13 = f32[5,2,8,128]{3,2,1,0:T(8,128)} copy(f32[5,2,8,128]{3,2,1,0:T(8,128)} %get-tuple-element.6) | data formatting | bytes 81920

commit v2 on v1

--- a/solution.py
+++ b/solution.py
@@ -33,11 +33,11 @@
 
     rhs_any, lower_any, upper_any, diag_any, pattern_any, counts_any, basis_any = take(7)
     precond_ref, coeffs_ref = take(2)
-    rhs_v, lower_v, upper_v, diag_v, pattern_v, counts_v, basis_v = take(7)
+    rhs_v, lower_v, upper_v, diag_v, counts_v, basis_v = take(6)
     gathered = take(levels - 1)
     outgoing = take(levels - 1)
     incoming = take(levels - 1)
-    pick = take(levels - 1)
+    (pattern_s,) = take(1)
     spread = take(levels - 1)
     (totals,) = take(1)
     load_sem, fwd_send, fwd_recv, bwd_send, bwd_recv, sum_send, sum_recv = take(7)
@@ -52,7 +52,7 @@
         return copy
 
     rhs_load = load(0, rhs_any, rhs_v)
-    pattern_load = load(1, pattern_any, pattern_v)
+    pattern_load = load(1, pattern_any, pattern_s)
     counts_load = load(2, counts_any, counts_v)
     lower_load = [
         load(3 + k, lower_any.at[k], lower_v.at[k]) for k in range(levels - 1)
@@ -94,36 +94,24 @@
     counts_load.wait()
     live = [
         [
-            (counts_v[k : k + 1, 0:1] > t).astype(jnp.float32)
+            (counts_v[0:1, k : k + 1] > t).astype(jnp.float32)
             for t in range(tiles)
         ]
         for k in range(levels)
     ]
 
+    def source(k, t, n):
+        return pattern_s[n, k, me * tiles + t]
+
     def selectors(k):
         span = gathered[k].shape[0]
-        table = pattern_v[k]
-        row = lax.broadcasted_iota(jnp.int32, table.shape, 0)
-        numbers = []
-        for t in range(tiles):
-            mine = jnp.sum(
-                jnp.where(row == me * tiles + t, table, 0), axis=0, keepdims=True
-            )
-            numbers += [mine[:, n : n + 1] for n in range(neighbours)]
-        lane_tile, lane_column = split(
-            lax.broadcasted_iota(jnp.int32, (columns, span * width), 1), columns
-        )
-        same = lane_column == lax.broadcasted_iota(jnp.int32, (columns, span * width), 0)
-        blocks = [
-            jnp.where(same & (lane_tile == number), 1.0, 0.0) for number in numbers
-        ]
-        pick[k][...] = jnp.concatenate(blocks, 0).astype(jnp.bfloat16)
         lane_pair, lane_column = split(
             lax.broadcasted_iota(jnp.int32, (1, pairs * columns), 1), columns
         )
         wanted = jnp.zeros((1, pairs * columns), jnp.int32)
-        for q, number in enumerate(numbers):
-            wanted = jnp.where(lane_pair == q, number, wanted)
+        for t in range(tiles):
+            for n in range(neighbours):
+                wanted = jnp.where(lane_pair == t * neighbours + n, source(k, t, n), wanted)
         row_tile, row_column = split(
             lax.broadcasted_iota(jnp.int32, (span * width, pairs * columns), 0), columns
         )
@@ -163,18 +151,23 @@
             selectors(k)
         lower_load[k - 1].wait()
         arrived(buffer, fwd_recv.at[k - 1], span)
-        picked = jnp.dot(
-            pick[k - 1][...],
-            buffer[...].reshape(span * width, rows),
-            preferred_element_type=jnp.float32,
-        ).astype(jnp.bfloat16)
+        picked = []
+        for t in range(tiles):
+            for n in range(neighbours):
+                owner, place = split(source(k - 1, t, n), tiles)
+                both = buffer[owner].astype(jnp.float32)
+                chosen = both[:columns]
+                for other in range(1, tiles):
+                    part = both[other * columns : (other + 1) * columns]
+                    chosen = jnp.where(place == other, part, chosen)
+                picked.append(chosen.astype(jnp.bfloat16))
         values = []
         for t in range(tiles):
             coupling = None
             for n in range(neighbours):
                 q = t * neighbours + n
                 term = lax.dot_general(
-                    picked[q * columns : (q + 1) * columns],
+                    picked[q],
                     lower_v[k - 1, t, n],
                     NT,
                     preferred_element_type=jnp.float32,
@@ -254,10 +247,12 @@
             project(k, values)
 
     lane = lax.broadcasted_iota(jnp.int32, (columns, rows), 1)
+    seat = lane - lax.broadcasted_iota(jnp.int32, (columns, rows), 0)
     packed = jnp.zeros((columns, rows), jnp.float32)
     for m, term in enumerate(partial + [squares]):
-        packed = jnp.where(lane == m, jnp.sum(term, axis=1, keepdims=True), packed)
-    totals[me] = packed
+        reduced = jnp.sum(term, axis=1, keepdims=True)
+        packed = jnp.where(seat == m * columns, reduced, packed)
+    totals[me] = jnp.sum(packed, axis=0, keepdims=True)
 
     def send(to_leaf, to_tile, index):
         pltpu.make_async_remote_copy(
@@ -275,7 +270,16 @@
         arrived(gathered[k - 1], fwd_send.at[k - 1], span)
         arrived(outgoing[k - 1], bwd_send.at[k - 1], span)
     arrived(totals, sum_recv, devices)
-    total = jnp.sum(totals[...], axis=0)
+    summed = jnp.broadcast_to(jnp.sum(totals[...], axis=0), (columns, rows))
+    spaced = jnp.where(split(lane, columns)[1] == lane - seat, summed, 0.0)
+    row_block, _ = split(lax.broadcasted_iota(jnp.int32, (rows, rows), 0), columns)
+    compress = row_block == lax.broadcasted_iota(jnp.int32, (rows, rows), 1)
+    total = jnp.dot(
+        spaced,
+        jnp.where(compress, 1.0, 0.0),
+        precision=lax.Precision.HIGHEST,
+        preferred_element_type=jnp.float32,
+    )
     squared = jnp.sum(jnp.where(lane == basis_size, total, 0.0), axis=1, keepdims=True)
     explained = jnp.sum(
         jnp.where(lane < basis_size, total * total, 0.0), axis=1, keepdims=True
@@ -283,7 +287,7 @@
     norm = jnp.sqrt(jnp.maximum(squared - explained, 0.0) + epsilon)
     scaled = norm / math.sqrt(levels * tiles * rows * devices)
     result = jnp.where(lane == basis_size, scaled, total)
-    coeffs_ref[...] = jnp.transpose(result)[: basis_size + 1]
+    coeffs_ref[...] = result[:, : basis_size + 1]
     arrived(totals, sum_send, devices)
 
 
@@ -295,28 +299,32 @@
     dims = (levels, tiles, columns, rows, neighbours, basis_size, n_leaf, n_tile)
     spans = [2 ** (k + 1) for k in range(1, levels)]
     width, pairs = tiles * columns, tiles * neighbours
+    pattern, counts = jnp.transpose(pattern, (2, 0, 1)), counts.T
     operands = (rhs, lower, upper, diag_inv, pattern, counts, basis)
     slots = [pltpu.VMEM((span, width, rows), jnp.bfloat16) for span in spans]
-    scratch = [pltpu.VMEM(operand.shape, operand.dtype) for operand in operands]
+    scratch = [
+        pltpu.VMEM(operand.shape, operand.dtype) for operand in operands if operand is not pattern
+    ]
     scratch += slots * 3
-    scratch += [pltpu.VMEM((pairs * columns, span * width), jnp.bfloat16) for span in spans]
+    scratch += [pltpu.SMEM(pattern.shape, pattern.dtype)]
     scratch += [pltpu.VMEM((span * width, pairs * columns), jnp.bfloat16) for span in spans]
-    scratch += [pltpu.VMEM((n_leaf * n_tile, columns, rows), jnp.float32)]
+    scratch += [pltpu.VMEM((n_leaf * n_tile, 1, rows), jnp.float32)]
     scratch += [pltpu.SemaphoreType.DMA((levels + 5,))]
     scratch += [pltpu.SemaphoreType.DMA((levels - 1,))] * 4
     scratch += [pltpu.SemaphoreType.DMA] * 2
-    return pl.pallas_call(
+    precond, coeffs = pl.pallas_call(
         functools.partial(kernel, dims),
         name="sweep",
         out_shape=(
             jax.ShapeDtypeStruct(rhs.shape, jnp.float32),
-            jax.ShapeDtypeStruct((basis_size + 1, columns), jnp.float32),
+            jax.ShapeDtypeStruct((columns, basis_size + 1), jnp.float32),
         ),
         in_specs=[pl.BlockSpec(memory_space=pl.ANY)] * len(operands),
         out_specs=[pl.BlockSpec(memory_space=pltpu.VMEM)] * 2,
         scratch_shapes=scratch,
         compiler_params=pltpu.CompilerParams(collective_id=0, has_side_effects=True),
     )(*operands)
+    return precond, coeffs.T
 
 
 def solution(mesh):

time: 52.4 us -> 47.6 us (0.908)
  local copies, waits for them, and re-layouts: 5.55 us -> 2 us
  Pallas kernels: 45.9 us -> 44.7 us
    unnamed x3 -> x4, local copies, waits for them, and re-layouts: 4.18 us -> 2 us
    pallas_call x1 -> x0, local copies, waits for them, and re-layouts: 1.36 us -> none  [local(): pl.pallas_call(functools.partial(kernel, dims), name='sweep', out_shape=(...]
    pallas_call x1, Pallas kernels: 45.9 us -> 44.7 us  [local(): pl.pallas_call(functools.partial(kernel, dims), name='sweep', out_shape=(...]
where the time goes in v2:
time: 47.6 us; the launch traced here: 47.4 us
  Pallas kernels  44.7 us (94%)
  local copies, waits for them, and re-layouts  2 us (4%)
  between operations  0.65 us (1%)
    pallas_call x1, Pallas kernels, local(): pl.pallas_call(functools.partial(kernel, dims), name='sweep', out_shape=(...  44.7 us
    unnamed x4, local copies, waits for them, and re-layouts  2 us

profile of v2, /device:TPU:0, one launch (start us, length us, event | category | flops | bytes accessed | tf_op | source)
XLA Modules:
  0.0 47.4 jit_solution(17914458643725261519)
XLA Ops:
  0.6 44.7 %sweep.1 = (f32[5,2,8,128]{3,2,1,0:T(8,128)}, f32[8,9]{1,0:T(8,128)}) custom-call(f32[5,2,8,128]{3,2,1,0:T(8,128)} %refs_0_.1, bf16[4,2,3,128,128]{4,3,2,1,0:T(8,128)(2,1)} %refs_1_.1, bf16[4,2,3,128,128]{4,3,2,1,0:T(8,128)(2,1)} %refs_2_.1, bf16[5,2,128,128]{3,2,1,0:T(8,128)(2,1)} %refs_3_.1, s32[3,4,64]{2,1,0:T(4,128)} %bitcast.3, s32[1,5]{1,0:T(1,128)} %bitcast.5, ...), custom_call_target="tpu_custom_call" | custom-call | tf_op jit(solution)/shard_map/sweep/pallas_call | solution.py:315
  45.4 0.0 copy-start
  45.4 1.4 %copy.11 = f32[5,2,8,128]{3,2,1,0:T(8,128)} copy(f32[5,2,8,128]{3,2,1,0:T(8,128)} %get-tuple-element.8) | data formatting | bytes 81920
  46.8 0.0 copy-done
  46.8 0.6 %copy.12 = f32[9,8]{0,1:T(8,128)} copy(f32[9,8]{0,1:T(8,128)S(1)} %bitcast.4) | data formatting | bytes 576
Async XLA Ops:
  45.4 1.4 %copy-start = (f32[8,9]{1,0:T(8,128)S(1)}, f32[8,9]{1,0:T(8,128)}, u32[]{:S(2)}) copy-start(f32[8,9]{1,0:T(8,128)} %get-tuple-element.5) | copy-start | bytes 868

commit v3 on v2

--- a/solution.py
+++ b/solution.py
@@ -41,6 +41,7 @@
     spread = take(levels - 1)
     (totals,) = take(1)
     load_sem, fwd_send, fwd_recv, bwd_send, bwd_recv, sum_send, sum_recv = take(7)
+    near_sem, far_sem = take(2)
 
     leaf = lax.axis_index("leaf")
     tile = lax.axis_index("tile")
@@ -83,14 +84,46 @@
             visit(leaf, other, own * n_tile + other)
 
     barrier = pltpu.get_barrier_semaphore()
-
-    def greet(to_leaf, to_tile, index):
-        pl.semaphore_signal(barrier, inc=1, device_id=(to_leaf, to_tile), device_id_type=MESH)
-
-    each_peer(n_leaf, greet)
+    beside = lax.div(leaf, 2) * 2 + lax.rem(leaf + 1, 2)
+
+    def greet(semaphore, to_leaf, to_tile):
+        pl.semaphore_signal(
+            semaphore, inc=1, device_id=(to_leaf, to_tile), device_id_type=MESH
+        )
+
+    greet(barrier, beside, 0)
+
+    @pl.when(tile == 0)
+    def _():
+        pl.semaphore_wait(barrier, 3)
+        greet(near_sem, leaf, 1)
+
+    @pl.when(tile == 1)
+    def _():
+        greet(barrier, leaf, 0)
+        pl.semaphore_wait(near_sem, 1)
+
+        def far(step, carry):
+            greet(barrier, lax.rem(leaf + step, n_leaf), 1)
+            return carry
+
+        if n_leaf <= 16:
+            for step in range(1, n_leaf):
+                far(step, 0)
+        else:
+            lax.fori_loop(1, n_leaf, far, 0)
+
+    def everyone_entered():
+        @pl.when(tile == 1)
+        def _():
+            pl.semaphore_wait(barrier, n_leaf - 1)
+            greet(far_sem, leaf, 0)
+
+        @pl.when(tile == 0)
+        def _():
+            pl.semaphore_wait(far_sem, 1)
 
     rhs_load.wait()
-    pattern_load.wait()
     counts_load.wait()
     live = [
         [
@@ -118,8 +151,6 @@
         chosen = (row_tile == wanted) & (row_column == lane_column)
         spread[k][...] = jnp.where(chosen, 1.0, 0.0).astype(jnp.bfloat16)
 
-    selectors(0)
-
     def group(k):
         span = gathered[k].shape[0]
         return span, lax.rem(me, span)
@@ -133,8 +164,8 @@
         buffer = gathered[k - 1]
         span, slot = group(k - 1)
         buffer[slot] = jnp.concatenate(forward_vals[-1], 0).astype(jnp.bfloat16)
-        if k == 1:
-            pl.semaphore_wait(barrier, devices - 1)
+        if k == 2:
+            everyone_entered()
 
         def send(to_leaf, to_tile, index):
             pltpu.make_async_remote_copy(
@@ -147,8 +178,9 @@
             ).start()
 
         each_peer(span // n_tile, send)
-        if k < levels - 1:
-            selectors(k)
+        if k == 1:
+            pattern_load.wait()
+        selectors(k - 1)
         lower_load[k - 1].wait()
         arrived(buffer, fwd_recv.at[k - 1], span)
         picked = []
@@ -312,6 +344,7 @@
     scratch += [pltpu.SemaphoreType.DMA((levels + 5,))]
     scratch += [pltpu.SemaphoreType.DMA((levels - 1,))] * 4
     scratch += [pltpu.SemaphoreType.DMA] * 2
+    scratch += [pltpu.SemaphoreType.REGULAR] * 2
     precond, coeffs = pl.pallas_call(
         functools.partial(kernel, dims),
         name="sweep",

time: 47.6 us -> 46.3 us (0.973)
  Pallas kernels: 44.7 us -> 43.5 us
    pallas_call x1, Pallas kernels: 44.7 us -> 43.5 us  [local(): pl.pallas_call(functools.partial(kernel, dims), name='sweep', out_shape=(...]
where the time goes in v3:
time: 46.3 us; the launch traced here: 46.1 us
  Pallas kernels  43.5 us (94%)
  local copies, waits for them, and re-layouts  2 us (4%)
  between operations  0.65 us (1%)
    pallas_call x1, Pallas kernels, local(): pl.pallas_call(functools.partial(kernel, dims), name='sweep', out_shape=(...  43.5 us
    unnamed x4, local copies, waits for them, and re-layouts  2 us

profile of v3, /device:TPU:0, one launch (start us, length us, event | category | flops | bytes accessed | tf_op | source)
XLA Modules:
  0.0 46.1 jit_solution(1147200852074263107)
XLA Ops:
  0.6 43.5 %sweep.1 = (f32[5,2,8,128]{3,2,1,0:T(8,128)}, f32[8,9]{1,0:T(8,128)}) custom-call(f32[5,2,8,128]{3,2,1,0:T(8,128)} %refs_0_.1, bf16[4,2,3,128,128]{4,3,2,1,0:T(8,128)(2,1)} %refs_1_.1, bf16[4,2,3,128,128]{4,3,2,1,0:T(8,128)(2,1)} %refs_2_.1, bf16[5,2,128,128]{3,2,1,0:T(8,128)(2,1)} %refs_3_.1, s32[3,4,64]{2,1,0:T(4,128)} %bitcast.3, s32[1,5]{1,0:T(1,128)} %bitcast.5, ...), custom_call_target="tpu_custom_call" | custom-call | tf_op jit(solution)/shard_map/sweep/pallas_call | solution.py:348
  44.1 0.0 copy-start
  44.1 1.4 %copy.11 = f32[5,2,8,128]{3,2,1,0:T(8,128)} copy(f32[5,2,8,128]{3,2,1,0:T(8,128)} %get-tuple-element.8) | data formatting | bytes 81920
  45.5 0.0 copy-done
  45.5 0.6 %copy.12 = f32[9,8]{0,1:T(8,128)} copy(f32[9,8]{0,1:T(8,128)S(1)} %bitcast.4) | data formatting | bytes 576
Async XLA Ops:
  44.1 1.4 %copy-start = (f32[8,9]{1,0:T(8,128)S(1)}, f32[8,9]{1,0:T(8,128)}, u32[]{:S(2)}) copy-start(f32[8,9]{1,0:T(8,128)} %get-tuple-element.5) | copy-start | bytes 868

commit v4 on v3

--- a/solution.py
+++ b/solution.py
@@ -41,7 +41,7 @@
     spread = take(levels - 1)
     (totals,) = take(1)
     load_sem, fwd_send, fwd_recv, bwd_send, bwd_recv, sum_send, sum_recv = take(7)
-    near_sem, far_sem = take(2)
+    near_sem, sibling_sem, far_sem = take(3)
 
     leaf = lax.axis_index("leaf")
     tile = lax.axis_index("tile")
@@ -84,7 +84,11 @@
             visit(leaf, other, own * n_tile + other)
 
     barrier = pltpu.get_barrier_semaphore()
-    beside = lax.div(leaf, 2) * 2 + lax.rem(leaf + 1, 2)
+    pair, odd = lax.div(leaf, 2), lax.rem(leaf, 2)
+    pair_count = n_leaf // 2
+    beside = pair * 2 + (1 - odd)
+    meets_sibling = (tile == 1) & (odd == 0)
+    meets_all = (tile == 1) & (odd == 1)
 
     def greet(semaphore, to_leaf, to_tile):
         pl.semaphore_signal(
@@ -103,25 +107,34 @@
         greet(barrier, leaf, 0)
         pl.semaphore_wait(near_sem, 1)
 
+    @pl.when(meets_sibling)
+    def _():
+        greet(barrier, (lax.div(pair, 2) * 2 + 1 - lax.rem(pair, 2)) * 2, 1)
+
+    @pl.when(meets_all)
+    def _():
         def far(step, carry):
-            greet(barrier, lax.rem(leaf + step, n_leaf), 1)
+            greet(barrier, lax.rem(pair + step, pair_count) * 2 + 1, 1)
             return carry
 
-        if n_leaf <= 16:
-            for step in range(1, n_leaf):
+        if pair_count <= 16:
+            for step in range(1, pair_count):
                 far(step, 0)
         else:
-            lax.fori_loop(1, n_leaf, far, 0)
-
-    def everyone_entered():
-        @pl.when(tile == 1)
+            lax.fori_loop(1, pair_count, far, 0)
+
+    def relay(heard, count, semaphore):
+        @pl.when(heard)
         def _():
-            pl.semaphore_wait(barrier, n_leaf - 1)
-            greet(far_sem, leaf, 0)
-
-        @pl.when(tile == 0)
+            pl.semaphore_wait(barrier, count)
+            greet(semaphore, beside, 0)
+            greet(semaphore, beside, 1)
+            greet(semaphore, leaf, 0)
+
+    def learn(heard, semaphore):
+        @pl.when(jnp.logical_not(heard))
         def _():
-            pl.semaphore_wait(far_sem, 1)
+            pl.semaphore_wait(semaphore, 1)
 
     rhs_load.wait()
     counts_load.wait()
@@ -165,7 +178,9 @@
         span, slot = group(k - 1)
         buffer[slot] = jnp.concatenate(forward_vals[-1], 0).astype(jnp.bfloat16)
         if k == 2:
-            everyone_entered()
+            learn(meets_sibling, sibling_sem)
+        if k == 3:
+            learn(meets_all, far_sem)
 
         def send(to_leaf, to_tile, index):
             pltpu.make_async_remote_copy(
@@ -181,6 +196,10 @@
         if k == 1:
             pattern_load.wait()
         selectors(k - 1)
+        if k == 1:
+            relay(meets_sibling, 1, sibling_sem)
+        if k == 2:
+            relay(meets_all, pair_count - 1, far_sem)
         lower_load[k - 1].wait()
         arrived(buffer, fwd_recv.at[k - 1], span)
         picked = []
@@ -344,7 +363,7 @@
     scratch += [pltpu.SemaphoreType.DMA((levels + 5,))]
     scratch += [pltpu.SemaphoreType.DMA((levels - 1,))] * 4
     scratch += [pltpu.SemaphoreType.DMA] * 2
-    scratch += [pltpu.SemaphoreType.REGULAR] * 2
+    scratch += [pltpu.SemaphoreType.REGULAR] * 3
     precond, coeffs = pl.pallas_call(
         functools.partial(kernel, dims),
         name="sweep",

time: 46.3 us -> 46.2 us (level)
  no operation moved by 1% of the time
where the time goes in v4:
time: 46.2 us; the launch traced here: 46 us
  Pallas kernels  43.4 us (94%)
  local copies, waits for them, and re-layouts  2 us (4%)
  between operations  0.65 us (1%)
    pallas_call x1, Pallas kernels, local(): pl.pallas_call(functools.partial(kernel, dims), name='sweep', out_shape=(...  43.4 us
    unnamed x4, local copies, waits for them, and re-layouts  2 us

profile of v4, /device:TPU:0, one launch (start us, length us, event | category | flops | bytes accessed | tf_op | source)
XLA Modules:
  0.0 46.0 jit_solution(12704062974110456857)
XLA Ops:
  0.6 43.4 %sweep.1 = (f32[5,2,8,128]{3,2,1,0:T(8,128)}, f32[8,9]{1,0:T(8,128)}) custom-call(f32[5,2,8,128]{3,2,1,0:T(8,128)} %refs_0_.1, bf16[4,2,3,128,128]{4,3,2,1,0:T(8,128)(2,1)} %refs_1_.1, bf16[4,2,3,128,128]{4,3,2,1,0:T(8,128)(2,1)} %refs_2_.1, bf16[5,2,128,128]{3,2,1,0:T(8,128)(2,1)} %refs_3_.1, s32[3,4,64]{2,1,0:T(4,128)} %bitcast.3, s32[1,5]{1,0:T(1,128)} %bitcast.5, ...), custom_call_target="tpu_custom_call" | custom-call | tf_op jit(solution)/shard_map/sweep/pallas_call | solution.py:367
  44.0 0.0 copy-start
  44.0 1.4 %copy.11 = f32[5,2,8,128]{3,2,1,0:T(8,128)} copy(f32[5,2,8,128]{3,2,1,0:T(8,128)} %get-tuple-element.8) | data formatting | bytes 81920
  45.4 0.0 copy-done
  45.4 0.6 %copy.12 = f32[9,8]{0,1:T(8,128)} copy(f32[9,8]{0,1:T(8,128)S(1)} %bitcast.4) | data formatting | bytes 576
Async XLA Ops:
  44.0 1.4 %copy-start = (f32[8,9]{1,0:T(8,128)S(1)}, f32[8,9]{1,0:T(8,128)}, u32[]{:S(2)}) copy-start(f32[8,9]{1,0:T(8,128)} %get-tuple-element.5) | copy-start | bytes 868
